TPU v7x, 32 devices: a whole 2x2x4 slice. The times are simulated.
32 devices in a mesh: row: 4 (over x, core), col: 8 (over z, y).
Axes of the slice: x: 2, y: 2, z: 4, core: 2. Of those that a mesh axis runs over, the one named last changes fastest.
Arguments:
- vectors: float32 [32768, 768], P(('row', 'col')), may hold values from -6 to 6
- list_ids: int32 [32768], P(('row', 'col')), may hold values from 0 to 16383, as said below
- pq_codes: int32 [32768, 96], P(('row', 'col')), may hold values from 0 to 255
- fill_counts: int32 [32, 32], P(('row', 'col')), may hold values from 0 to 32, as said below
- centroids: float32 [16384, 768], P(('row', 'col')), may hold values from -6 to 6
- codebook: float32 [96, 8, 256], P('col'), may hold values from -6 to 6
Outputs:
- coded_err: float32 [32768], P(('row', 'col'))
- best_err: float32 [32768], P(('row', 'col'))
Inputs may be any that keep to these rules, and one draw needn't show every extreme that they name: `list_ids`: slot s of device p lies in block s // 32, which belongs to owner device s // 32 (devices numbered row-major over row and col); it names a list of that owner, from (s // 32) * 512 to (s // 32 + 1) * 512 - 1. fill_counts[p, d] is the number of live slots at the head of device p's block for owner d; some owner receives 32 live slots from every device.
All inputs are finite; a program needn't handle non-finite values.
Results may differ from a plain program's by a relative error of at most 0.0003.
Values sent between devices are 32-bit elements; how exact they have to be, the bound alone decides.
A program may use at most 256 MiB of HBM per device.

v0:
```python
import jax
import jax.numpy as jnp
from jax import lax
from jax.sharding import PartitionSpec as P


def block_terms(block_vec, block_codes, shard_piece, code_norms):
    resid_norms = jnp.sum(block_vec * block_vec, axis=2)
    cross_term = jnp.einsum("bms,msk->bmk", block_vec, shard_piece, precision=lax.Precision.HIGHEST)
    dist_table = resid_norms[:, :, None] - 2.0 * cross_term + code_norms[None, :, :]
    best_sum = jnp.sum(jnp.min(dist_table, axis=2), axis=1)
    code_index = lax.broadcasted_iota(jnp.int32, dist_table.shape, 2)
    coded_sum = jnp.sum(
        jnp.where(code_index == block_codes[:, :, None], dist_table, 0.0), axis=(1, 2)
    )
    return jnp.stack([coded_sum, best_sum])


def local(vectors, list_ids, pq_codes, fill_counts, centroids, codebook):
    row_count = lax.axis_size("row")
    col_count = lax.axis_size("col")
    device_count = row_count * col_count
    slot_count = vectors.shape[0]
    capacity = slot_count // device_count
    feature_width = vectors.shape[1]
    sub_total = pq_codes.shape[1]
    sub_width = feature_width // sub_total
    out_vec = vectors.reshape(device_count, capacity, feature_width)
    out_ids = list_ids.reshape(device_count, capacity)
    out_codes = pq_codes.reshape(device_count, capacity, sub_total)
    got_vec, got_ids, got_codes = (
        lax.all_to_all(out_vec, ("row", "col"), split_axis=0, concat_axis=0, tiled=True),
        lax.all_to_all(out_ids, ("row", "col"), split_axis=0, concat_axis=0, tiled=True),
        lax.all_to_all(out_codes, ("row", "col"), split_axis=0, concat_axis=0, tiled=True),
    )
    got_vec = got_vec.reshape(slot_count, feature_width)
    got_ids = got_ids.reshape(slot_count)
    got_codes = got_codes.reshape(slot_count, sub_total)
    residual = got_vec - jnp.take(centroids, got_ids % centroids.shape[0], axis=0)
    block_rows = 128
    block_count = slot_count // block_rows
    shard_piece = lax.all_gather(codebook, "col", axis=0, tiled=True)
    sub_count = shard_piece.shape[0]
    code_norms = jnp.sum(shard_piece * shard_piece, axis=1)
    shaped = residual.reshape(block_count, block_rows, sub_count, sub_width)
    shaped_codes = got_codes.reshape(block_count, block_rows, sub_count)

    def one_block(pair):
        return block_terms(pair[0], pair[1], shard_piece, code_norms)

    parts = lax.map(one_block, (shaped, shaped_codes))
    totals = jnp.transpose(parts, (1, 0, 2)).reshape(2, slot_count)
    coded_sum = totals[0]
    best_sum = totals[1]
    back_coded, back_best = (
        lax.all_to_all(
            coded_sum.reshape(device_count, capacity),
            ("row", "col"),
            split_axis=0,
            concat_axis=0,
            tiled=True,
        ),
        lax.all_to_all(
            best_sum.reshape(device_count, capacity),
            ("row", "col"),
            split_axis=0,
            concat_axis=0,
            tiled=True,
        ),
    )
    slot_pos = jnp.arange(capacity, dtype=jnp.int32)
    live_mask = slot_pos[None, :] < fill_counts[0][:, None]
    coded_err = jnp.where(live_mask, back_coded, 0.0).reshape(slot_count)
    best_err = jnp.where(live_mask, back_best, 0.0).reshape(slot_count)
    return (coded_err, best_err)


def solution(mesh):
    in_specs = (
        P(("row", "col"), None),
        P(("row", "col")),
        P(("row", "col"), None),
        P(("row", "col"), None),
        P(("row", "col"), None),
        P("col", None, None),
    )
    out_specs = (P(("row", "col")), P(("row", "col")))
    return jax.shard_map(local, mesh=mesh, in_specs=in_specs, out_specs=out_specs, check_vma=False)
```

profile of v0, /device:TPU:13, one launch (start us, length us, event | category | flops | bytes accessed | tf_op | source)
XLA Modules:
  0.0 353.3 jit_solution(16546367469108765368)
XLA Ops:
  0.6 0.0 copy-start
  0.6 1.5 all_to_all.30
  2.1 6.3 %all-to-all-start.2 = ((s32[32,1,32]{2,1,0:T(1,128)}), s32[32,1,32]{2,1,0:T(1,128)S(1)}, u32[]{:S(2)}, u32[]{:S(2)}) async-start(s32[32,1,32]{2,1,0:T(1,128)} %all_to_all.30), calls=%async_computation.2 | async-start | bytes 32768 | tf_op jit(solution)/shard_map/all_to_all | solution.py:33
  8.4 1.2 copy.14
  9.6 3.6 %all-to-all-done.2 = s32[32,1,32]{2,1,0:T(1,128)S(1)} async-done(((s32[32,1,32]{2,1,0:T(1,128)}), s32[32,1,32]{2,1,0:T(1,128)S(1)}, u32[]{:S(2)}, u32[]{:S(2)}) %all-to-all-start.2) | async-done | bytes 4128 | tf_op jit(solution)/shard_map/all_to_all | solution.py:33
  13.2 17.6 %all_to_all.43 = s32[32,32,96]{2,1,0:T(8,128)S(1)} all-to-all(s32[32,32,96]{2,1,0:T(8,128)S(1)} %bitcast.59), channel_id=1, replica_groups=mesh['row'=4,'col'=8] {'row','col'}, dimensions={0} | all-to-all | bytes 786432 | tf_op jit(solution)/shard_map/all_to_all | solution.py:34
  30.8 0.0 copy-start.1
  30.8 6.3 %all-to-all-start.1 = ((f32[32,32,768]{2,1,0:T(8,128)}), f32[32,32,768]{2,1,0:T(8,128)}, u32[]{:S(2)}, u32[]{:S(2)}) async-start(f32[32,32,768]{2,1,0:T(8,128)} %bitcast.57), calls=%async_computation.1 | async-start | bytes 6291456 | tf_op jit(solution)/shard_map/all_to_all | solution.py:32
  37.1 0.0 copy-done.1
  37.1 87.1 %all_gather.3 = f32[96,8,256]{2,1,0:T(8,128)S(1)} all-gather(f32[12,8,256]{2,1,0:T(8,128)S(1)} %copy-done.1), channel_id=1, replica_groups=mesh['row'=4,'col'=8] {'col'}, dimensions={0}, use_global_device_ids=true | all-gather | bytes 884736 | tf_op jit(solution)/shard_map/all_gather | solution.py:42
  124.1 0.2 multiply_reduce_fusion.1
  124.4 0.1 reshape.128
  124.5 0.0 copy-done
  124.5 5.3 %gather_fusion = f32[1024,768]{1,0:T(8,128)} fusion(f32[512,768]{1,0:T(8,128)S(1)} %copy-done, s32[1024]{0:T(1024)S(1)} %broadcast_clamp_fusion), kind=kCustom, calls=%fused_computation | custom fusion | bytes 6295552 | tf_op jit(solution)/shard_map/jit(_take)/gather | solution.py:39
  129.8 3.6 %copy.16 = f32[1024,768]{0,1:T(8,128)} copy(f32[1024,768]{1,0:T(8,128)} %gather_fusion) | data formatting | bytes 6291456 | tf_op jit(solution)/shard_map/jit(_take)/gather | solution.py:39
  133.3 0.5 broadcast.130
  133.8 0.7 reduce.19
  134.5 0.1 reshape.127
  134.6 0.2 copy.17
  134.8 0.0 all-to-all-done.1
  134.8 11.3 %copy.15 = f32[32,32,768]{1,0,2:T(8,128)} copy(f32[32,32,768]{2,1,0:T(8,128)} %all-to-all-done.1) | data formatting | bytes 6291456 | tf_op jit(solution)/shard_map/all_to_all | solution.py:32
  146.2 9.4 %reshape.126 = f32[8,128,96,8]{1,0,3,2:T(8,128)} reshape(f32[32,32,768]{1,0,2:T(8,128)} %copy.15) | data formatting | bytes 6291456 | tf_op jit(solution)/shard_map/reshape | solution.py:36
  155.6 5.7 %fusion.3 = f32[8,128,96,8]{1,0,3,2:T(8,128)} fusion(f32[8,128,96,8]{1,0,3,2:T(8,128)} %reshape.126, f32[96,8,8,128]{3,1,2,0:T(8,128)} %bitcast.56, pred[8,128]{1,0:T(8,128)(4,1)S(1)} %compare_and_fusion), kind=kLoop, calls=%fused_computation.12 | loop fusion | flops 1572864 | bytes 9438208 | tf_op jit(solution)/shard_map/sub | solution.py:39
  161.2 0.0 copy-start.2
  161.2 165.1 %while.10 = (s32[]{:T(128)}, f32[8,2,128]{2,1,0:T(2,128)S(1)}, s32[8,128,96]{1,2,0:T(8,128)S(1)}, f32[8,128,96,8]{1,0,3,2:T(8,128)}, f32[96,8,256]{2,1,0:T(8,128...) while((s32[]{:T(128)}, f32[8,2,128]{2,1,0:T(2,128)S(1)}, s32[8,128,96]{1,2,0:T(8,128)S(1)}, ...), condition=%wide.region_6.7_spmd, body=%wide.region_1.0_spmd.sunk | while | flops 324194304 | bytes 2804845 | solution.py:51
  161.2 2.3 constant_dynamic-slice_fusion.2
  163.5 0.1 multiply_reduce_fusion.3
  163.7 18.2 %select_reduce_fusion.2 = (f32[128]{0:T(128)S(1)}, f32[128,96]{0,1:T(8,128)S(1)}) fusion(f32[96,256]{1,0:T(8,128)S(1)} %get-tuple-element.127, f32[128,96]{0,1:T(8,128)S(1)} %multiply_reduce_fusion.3, s32[128,96]{0,1:T(8,128)S(1)} %dynamic-slice_bitcast_fusion.2, f32[128,96,8]{0,2,1:T(8,128)S(1)} %bitcast.55, f32[96,8,256]{2,1,0:T(8,128)S(1)} %get-tuple-element.126), kind=kOutput, calls=%fused_computation.3.clone.1 | convolution fusion | flops 323997568 | bytes 1425920 | tf_op jit(solution)/shard_map/while/body/eval_jaxpr/bms,msk->bmk/dot_general | solution.py:9
  181.9 2.3 constant_dynamic-slice_fusion.2
  184.2 0.1 multiply_reduce_fusion.3
  184.3 18.2 %select_reduce_fusion.2 = (f32[128]{0:T(128)S(1)}, f32[128,96]{0,1:T(8,128)S(1)}) fusion(f32[96,256]{1,0:T(8,128)S(1)} %get-tuple-element.127, f32[128,96]{0,1:T(8,128)S(1)} %multiply_reduce_fusion.3, s32[128,96]{0,1:T(8,128)S(1)} %dynamic-slice_bitcast_fusion.2, f32[128,96,8]{0,2,1:T(8,128)S(1)} %bitcast.55, f32[96,8,256]{2,1,0:T(8,128)S(1)} %get-tuple-element.126), kind=kOutput, calls=%fused_computation.3.clone.1 | convolution fusion | flops 323997568 | bytes 1425920 | tf_op jit(solution)/shard_map/while/body/eval_jaxpr/bms,msk->bmk/dot_general | solution.py:9
  202.5 2.3 constant_dynamic-slice_fusion.2
  204.8 0.1 multiply_reduce_fusion.3
  204.9 18.2 %select_reduce_fusion.2 = (f32[128]{0:T(128)S(1)}, f32[128,96]{0,1:T(8,128)S(1)}) fusion(f32[96,256]{1,0:T(8,128)S(1)} %get-tuple-element.127, f32[128,96]{0,1:T(8,128)S(1)} %multiply_reduce_fusion.3, s32[128,96]{0,1:T(8,128)S(1)} %dynamic-slice_bitcast_fusion.2, f32[128,96,8]{0,2,1:T(8,128)S(1)} %bitcast.55, f32[96,8,256]{2,1,0:T(8,128)S(1)} %get-tuple-element.126), kind=kOutput, calls=%fused_computation.3.clone.1 | convolution fusion | flops 323997568 | bytes 1425920 | tf_op jit(solution)/shard_map/while/body/eval_jaxpr/bms,msk->bmk/dot_general | solution.py:9
  223.2 2.3 constant_dynamic-slice_fusion.2
  225.4 0.1 multiply_reduce_fusion.3
  225.6 18.2 %select_reduce_fusion.2 = (f32[128]{0:T(128)S(1)}, f32[128,96]{0,1:T(8,128)S(1)}) fusion(f32[96,256]{1,0:T(8,128)S(1)} %get-tuple-element.127, f32[128,96]{0,1:T(8,128)S(1)} %multiply_reduce_fusion.3, s32[128,96]{0,1:T(8,128)S(1)} %dynamic-slice_bitcast_fusion.2, f32[128,96,8]{0,2,1:T(8,128)S(1)} %bitcast.55, f32[96,8,256]{2,1,0:T(8,128)S(1)} %get-tuple-element.126), kind=kOutput, calls=%fused_computation.3.clone.1 | convolution fusion | flops 323997568 | bytes 1425920 | tf_op jit(solution)/shard_map/while/body/eval_jaxpr/bms,msk->bmk/dot_general | solution.py:9
  243.8 2.3 constant_dynamic-slice_fusion.2
  246.1 0.1 multiply_reduce_fusion.3
  246.2 18.2 %select_reduce_fusion.2 = (f32[128]{0:T(128)S(1)}, f32[128,96]{0,1:T(8,128)S(1)}) fusion(f32[96,256]{1,0:T(8,128)S(1)} %get-tuple-element.127, f32[128,96]{0,1:T(8,128)S(1)} %multiply_reduce_fusion.3, s32[128,96]{0,1:T(8,128)S(1)} %dynamic-slice_bitcast_fusion.2, f32[128,96,8]{0,2,1:T(8,128)S(1)} %bitcast.55, f32[96,8,256]{2,1,0:T(8,128)S(1)} %get-tuple-element.126), kind=kOutput, calls=%fused_computation.3.clone.1 | convolution fusion | flops 323997568 | bytes 1425920 | tf_op jit(solution)/shard_map/while/body/eval_jaxpr/bms,msk->bmk/dot_general | solution.py:9
  264.4 2.3 constant_dynamic-slice_fusion.2
  266.7 0.1 multiply_reduce_fusion.3
  266.9 18.2 %select_reduce_fusion.2 = (f32[128]{0:T(128)S(1)}, f32[128,96]{0,1:T(8,128)S(1)}) fusion(f32[96,256]{1,0:T(8,128)S(1)} %get-tuple-element.127, f32[128,96]{0,1:T(8,128)S(1)} %multiply_reduce_fusion.3, s32[128,96]{0,1:T(8,128)S(1)} %dynamic-slice_bitcast_fusion.2, f32[128,96,8]{0,2,1:T(8,128)S(1)} %bitcast.55, f32[96,8,256]{2,1,0:T(8,128)S(1)} %get-tuple-element.126), kind=kOutput, calls=%fused_computation.3.clone.1 | convolution fusion | flops 323997568 | bytes 1425920 | tf_op jit(solution)/shard_map/while/body/eval_jaxpr/bms,msk->bmk/dot_general | solution.py:9
  285.1 2.3 constant_dynamic-slice_fusion.2
  287.4 0.1 multiply_reduce_fusion.3
  287.5 18.2 %select_reduce_fusion.2 = (f32[128]{0:T(128)S(1)}, f32[128,96]{0,1:T(8,128)S(1)}) fusion(f32[96,256]{1,0:T(8,128)S(1)} %get-tuple-element.127, f32[128,96]{0,1:T(8,128)S(1)} %multiply_reduce_fusion.3, s32[128,96]{0,1:T(8,128)S(1)} %dynamic-slice_bitcast_fusion.2, f32[128,96,8]{0,2,1:T(8,128)S(1)} %bitcast.55, f32[96,8,256]{2,1,0:T(8,128)S(1)} %get-tuple-element.126), kind=kOutput, calls=%fused_computation.3.clone.1 | convolution fusion | flops 323997568 | bytes 1425920 | tf_op jit(solution)/shard_map/while/body/eval_jaxpr/bms,msk->bmk/dot_general | solution.py:9
  305.7 2.3 constant_dynamic-slice_fusion.2
  308.0 0.1 multiply_reduce_fusion.3
  308.1 18.2 %select_reduce_fusion.2 = (f32[128]{0:T(128)S(1)}, f32[128,96]{0,1:T(8,128)S(1)}) fusion(f32[96,256]{1,0:T(8,128)S(1)} %get-tuple-element.127, f32[128,96]{0,1:T(8,128)S(1)} %multiply_reduce_fusion.3, s32[128,96]{0,1:T(8,128)S(1)} %dynamic-slice_bitcast_fusion.2, f32[128,96,8]{0,2,1:T(8,128)S(1)} %bitcast.55, f32[96,8,256]{2,1,0:T(8,128)S(1)} %get-tuple-element.126), kind=kOutput, calls=%fused_computation.3.clone.1 | convolution fusion | flops 323997568 | bytes 1425920 | tf_op jit(solution)/shard_map/while/body/eval_jaxpr/bms,msk->bmk/dot_general | solution.py:9
  326.4 0.7 all_to_all.35
  327.1 10.4 %all-to-all-start.4 = ((f32[32,1,32]{2,1,0:T(1,128)}), f32[32,1,32]{2,1,0:T(1,128)S(1)}, u32[]{:S(2)}, u32[]{:S(2)}) async-start(f32[32,1,32]{2,1,0:T(1,128)} %all_to_all.35), calls=%async_computation.4 | async-start | bytes 32768 | tf_op jit(solution)/shard_map/all_to_all | solution.py:63
  337.5 0.7 all_to_all.32
  338.2 4.1 %all-to-all-done.4 = f32[32,1,32]{2,1,0:T(1,128)S(1)} async-done(((f32[32,1,32]{2,1,0:T(1,128)}), f32[32,1,32]{2,1,0:T(1,128)S(1)}, u32[]{:S(2)}, u32[]{:S(2)}) %all-to-all-start.4) | async-done | bytes 4128 | tf_op jit(solution)/shard_map/all_to_all | solution.py:63
  342.3 4.8 %all-to-all-start.3 = ((f32[32,1,32]{2,1,0:T(1,128)}), f32[32,1,32]{2,1,0:T(1,128)S(1)}, u32[]{:S(2)}, u32[]{:S(2)}) async-start(f32[32,1,32]{2,1,0:T(1,128)} %all_to_all.32), calls=%async_computation.3 | async-start | bytes 32768 | tf_op jit(solution)/shard_map/all_to_all | solution.py:56
  347.1 0.0 copy-done.2
  347.1 0.1 iota_compare_fusion.1
  347.2 0.1 lt.53
  347.3 0.5 broadcast.131
  347.8 0.7 reduce.21
  348.5 0.1 all_to_all.37
  348.5 3.4 all-to-all-done.3
  351.9 0.7 reduce.20
  352.6 0.1 all_to_all.34
  352.7 0.6 broadcast_select_fusion
  (29 shorter events, 0.6 us)
Async XLA Ops:
  0.6 123.9 %copy-start = (f32[512,768]{1,0:T(8,128)S(1)}, f32[512,768]{1,0:T(8,128)}, u32[]{:S(2)}) copy-start(f32[512,768]{1,0:T(8,128)} %param.12) | copy-start | bytes 4718596
  2.1 11.1 %all-to-all-start.2 = ((s32[32,1,32]{2,1,0:T(1,128)}), s32[32,1,32]{2,1,0:T(1,128)S(1)}, u32[]{:S(2)}, u32[]{:S(2)}) async-start(s32[32,1,32]{2,1,0:T(1,128)} %all_to_all.30), calls=%async_computation.2 | async-start | bytes 32768 | tf_op jit(solution)/shard_map/all_to_all | solution.py:33
  30.8 6.3 %copy-start.1 = (f32[12,8,256]{2,1,0:T(8,128)S(1)}, f32[12,8,256]{2,1,0:T(8,128)}, u32[]{:S(2)}) copy-start(f32[12,8,256]{2,1,0:T(8,128)} %param.13) | copy-start | bytes 294916
  30.8 104.0 %all-to-all-start.1 = ((f32[32,32,768]{2,1,0:T(8,128)}), f32[32,32,768]{2,1,0:T(8,128)}, u32[]{:S(2)}, u32[]{:S(2)}) async-start(f32[32,32,768]{2,1,0:T(8,128)} %bitcast.57), calls=%async_computation.1 | async-start | bytes 6291456 | tf_op jit(solution)/shard_map/all_to_all | solution.py:32
  161.2 185.8 %copy-start.2 = (s32[1,32]{1,0:T(1,128)S(1)}, s32[1,32]{1,0:T(1,128)}, u32[]{:S(2)}) copy-start(s32[1,32]{1,0:T(1,128)} %param.11) | copy-start | bytes 388
  327.1 15.2 %all-to-all-start.4 = ((f32[32,1,32]{2,1,0:T(1,128)}), f32[32,1,32]{2,1,0:T(1,128)S(1)}, u32[]{:S(2)}, u32[]{:S(2)}) async-start(f32[32,1,32]{2,1,0:T(1,128)} %all_to_all.35), calls=%async_computation.4 | async-start | bytes 32768 | tf_op jit(solution)/shard_map/all_to_all | solution.py:63
  342.3 9.6 %all-to-all-start.3 = ((f32[32,1,32]{2,1,0:T(1,128)}), f32[32,1,32]{2,1,0:T(1,128)S(1)}, u32[]{:S(2)}, u32[]{:S(2)}) async-start(f32[32,1,32]{2,1,0:T(1,128)} %all_to_all.32), calls=%async_computation.3 | async-start | bytes 32768 | tf_op jit(solution)/shard_map/all_to_all | solution.py:56
where the time goes:
time: 358 us; the launch traced here: 353 us
  matrix products  145 us (41%)
  blocking collectives  105 us (29%)
  local copies, waits for them, and re-layouts  53.5 us (15%)
  starting transfers between devices  27.7 us (8%)
  waiting for transfers between devices  11.1 us (3%)
  other arithmetic  9.97 us (3%)
    dot_general x8, matrix products, block_terms(): jnp.einsum('bms,msk->bmk', block_vec, shard_piece, precision=lax.Precisio...  145 us
    all_gather x1, blocking collectives, local(): shard_piece = lax.all_gather(codebook, 'col', axis=0, tiled=True)  87.1 us
    dynamic_slice x8, local copies, waits for them, and re-layouts, local(): parts = lax.map(one_block, (shaped, shaped_codes))  18.1 us
    all_to_all x1, blocking collectives, local(): lax.all_to_all(out_codes, ('row', 'col'), split_axis=0, concat_axis=0, ti...  17.6 us
    all_to_all x1, local copies, waits for them, and re-layouts, local(): lax.all_to_all(out_vec, ('row', 'col'), split_axis=0, concat_axis=0, tile...  11.3 us
    all_to_all x1, starting transfers between devices, local(): lax.all_to_all(best_sum.reshape(device_count, capacity), ('row', 'col'),...  10.4 us
    reshape x1, local copies, waits for them, and re-layouts, local(): got_vec = got_vec.reshape(slot_count, feature_width)  9.42 us
    gather x2, local copies, waits for them, and re-layouts, local(): jnp.take(centroids, got_ids % centroids.shape[0], axis=0)  8.83 us
  transfers between devices with their start and end apart: 4, of which 3 were waited for; matrix products, arithmetic and copies ran while one was open for 4% of the time, Pallas kernels for 0%

commit v1 on v0

v1 whole, which is shorter than its diff:
```python
import functools

import jax
import jax.numpy as jnp
from jax import lax
from jax.experimental import pallas as pl
from jax.experimental.pallas import tpu as pltpu
from jax.sharding import PartitionSpec as P

F32 = jnp.float32
BF16 = jnp.bfloat16
DEPTH = 64


def split3(x):
    hi = x.astype(BF16).astype(F32)
    rest = x - hi
    mid = rest.astype(BF16).astype(F32)
    return hi, mid, rest - mid


def build_table(cb_ref, w_ref):
    sub_count, sub_width, code_count = cb_ref.shape

    def step(m, carry):
        c = cb_ref[m]
        hi, mid, lo = split3(-2.0 * c)
        norm = jnp.sum(c * c, axis=0, keepdims=True)
        nh, nm, nl = split3(norm)
        line = lax.broadcasted_iota(jnp.int32, c.shape, 0)
        norms = jnp.where(line == 0, nh, jnp.where(line == 1, nm, jnp.where(line == 2, nl, 0.0)))
        pieces = [hi, hi, hi, mid, mid, lo, norms, jnp.zeros_like(c)]
        w_ref[m] = jnp.concatenate(pieces, axis=0).T.astype(BF16)
        return carry

    lax.fori_loop(0, sub_count, step, 0, unroll=4)


def pick(row, code, sub_width):
    lanes = code.shape[1]
    outs = []
    for start in range(0, lanes, 128):
        idx = jnp.broadcast_to(code[:, start:start + 128], (sub_width, 128))
        low = jnp.bitwise_and(idx, 127)
        got = None
        for part in range(row.shape[1] // 128):
            piece = jnp.take_along_axis(
                row[:, part * 128:(part + 1) * 128], low, axis=1, mode="promise_in_bounds"
            )
            got = piece if got is None else jnp.where(idx >= part * 128, piece, got)
        outs.append(got)
    return jnp.concatenate(outs, axis=1)


def score(rt_ref, codes_ref, cb_ref, w_ref, unroll):
    sub_count, sub_width, code_count = cb_ref.shape
    width = rt_ref.shape[1]
    ones = jnp.ones((sub_width, width), F32)
    zeros = jnp.zeros((sub_width, width), F32)

    def step(m, carry):
        coded, norm, best = carry
        r = rt_ref[pl.ds(pl.multiple_of(m * sub_width, sub_width), sub_width), :]
        hi, mid, lo = split3(r)
        x = jnp.concatenate([hi, mid, lo, hi, mid, hi, ones, zeros], axis=0).astype(BF16)
        table = jnp.dot(w_ref[m], x, preferred_element_type=F32)
        best = best + jnp.min(table, axis=0, keepdims=True)
        norm = norm + r * r
        diff = r - pick(cb_ref[m], codes_ref[pl.ds(m, 1), :], sub_width)
        return coded + diff * diff, norm, best

    coded, norm, best = lax.fori_loop(
        0, sub_count, step, (zeros, zeros, jnp.zeros((1, width), F32)), unroll=unroll
    )
    coded = jnp.sum(coded, axis=0, keepdims=True)
    best = best + jnp.sum(norm, axis=0, keepdims=True)
    return coded, best


def score_kernel(v_ref, c_ref, codes_ref, cb_ref, w_ref, coded_ref, best_ref, rt_ref):
    rt_ref[...] = (v_ref[...] - c_ref[...]).T
    coded, best = score(rt_ref, codes_ref, cb_ref, w_ref, 4)
    coded_ref[...] = coded
    best_ref[...] = best


def local(vectors, list_ids, pq_codes, fill_counts, centroids, codebook):
    row_count = lax.axis_size("row")
    col_count = lax.axis_size("col")
    device_count = row_count * col_count
    slot_count, feature_width = vectors.shape
    capacity = slot_count // device_count
    sub_total = pq_codes.shape[1]
    sub_width, code_count = codebook.shape[1:]
    axes = ("row", "col")
    swap = functools.partial(lax.all_to_all, axis_name=axes, split_axis=0, concat_axis=0, tiled=True)

    got_ids = swap(list_ids.reshape(device_count, capacity)).reshape(slot_count)
    wanted = jnp.take(centroids, got_ids % centroids.shape[0], axis=0, mode="clip")
    share = sub_width // row_count
    mine = lax.dynamic_slice_in_dim(codebook, lax.axis_index("row") * share, share, axis=1)
    mine = lax.all_gather(mine, "col", axis=0, tiled=True)
    book = lax.all_gather(mine, "row", axis=1, tiled=True)
    got_cent = swap(wanted.reshape(device_count, capacity, feature_width)).reshape(slot_count, feature_width)
    codes_t = pq_codes.T

    table = pl.pallas_call(
        build_table,
        out_shape=jax.ShapeDtypeStruct((sub_total, code_count, DEPTH), BF16),
        in_specs=[pl.BlockSpec(memory_space=pltpu.VMEM)],
        out_specs=pl.BlockSpec(memory_space=pltpu.VMEM),
        cost_estimate=pl.CostEstimate(flops=10**8, bytes_accessed=20_000_000, transcendentals=0),
        name="build_table",
    )(book)

    width = 256
    whole3 = lambda i: (0, 0, 0)
    coded, best = pl.pallas_call(
        score_kernel,
        grid=(slot_count // width,),
        out_shape=[jax.ShapeDtypeStruct((1, slot_count), F32)] * 2,
        in_specs=[
            pl.BlockSpec((width, feature_width), lambda i: (i, 0)),
            pl.BlockSpec((width, feature_width), lambda i: (i, 0)),
            pl.BlockSpec((sub_total, width), lambda i: (0, i)),
            pl.BlockSpec((sub_total, sub_width, code_count), whole3),
            pl.BlockSpec((sub_total, code_count, DEPTH), whole3),
        ],
        out_specs=[pl.BlockSpec((1, width), lambda i: (0, i))] * 2,
        scratch_shapes=[pltpu.VMEM((feature_width, width), F32)],
        name="score",
    )(vectors, got_cent, codes_t, book, table)

    slot_pos = jnp.arange(capacity, dtype=jnp.int32)
    live = (slot_pos[None, :] < fill_counts[0][:, None]).reshape(slot_count)
    coded_err = jnp.where(live, coded.reshape(slot_count), 0.0)
    best_err = jnp.where(live, best.reshape(slot_count), 0.0)
    return (coded_err, best_err)


def solution(mesh):
    in_specs = (
        P(("row", "col"), None),
        P(("row", "col")),
        P(("row", "col"), None),
        P(("row", "col"), None),
        P(("row", "col"), None),
        P("col", None, None),
    )
    out_specs = (P(("row", "col")), P(("row", "col")))
    return jax.shard_map(local, mesh=mesh, in_specs=in_specs, out_specs=out_specs, check_vma=False)
```

time: 358 us -> 170 us (0.47)
  the two profiles are of different devices: /device:TPU:13 before, /device:TPU:0 now
where the time goes in v1:
time: 170 us
  blocking collectives  114 us (67%)
  Pallas kernels  40.6 us (24%)
  local copies, waits for them, and re-layouts  9.14 us (5%)
  starting transfers between devices  3.67 us (2%)
  other arithmetic  2.09 us (1%)
    all_gather x1, blocking collectives, local(): mine = lax.all_gather(mine, 'col', axis=0, tiled=True)  90.9 us
    pallas_call x1, Pallas kernels, local(): pl.pallas_call(score_kernel, grid=(slot_count // width,), out_shape=[jax....  33.4 us
    all_to_all x1, blocking collectives, local(): got_ids = swap(list_ids.reshape(device_count, capacity)).reshape(slot_count)  14.3 us
    all_gather x1, blocking collectives, local(): book = lax.all_gather(mine, 'row', axis=1, tiled=True)  8.52 us
    pallas_call x1, Pallas kernels, local(): pl.pallas_call(build_table, out_shape=jax.ShapeDtypeStruct((sub_total, co...  7.16 us
    gather x1, local copies, waits for them, and re-layouts, local(): jnp.take(centroids, got_ids % centroids.shape[0], axis=0, mode='clip')  5.26 us
    all_to_all x1, starting transfers between devices, local(): swap(wanted.reshape(device_count, capacity, feature_width))  3.67 us
  transfers between devices with their start and end apart: 1, of which 0 were waited for; matrix products, arithmetic and copies ran while one was open for 1% of the time, Pallas kernels for 4%

profile of v1, /device:TPU:0, one launch (start us, length us, event | category | flops | bytes accessed | tf_op | source)
XLA Modules:
  0.0 169.8 jit_solution(11072605537768782579)
XLA Ops:
  0.6 0.0 copy-start
  0.6 0.9 all_to_all.9
  1.5 14.3 %all_to_all.14 = s32[32,1,32]{2,1,0:T(1,128)S(1)} all-to-all(s32[32,1,32]{2,1,0:T(1,128)S(1)} %all_to_all.9), channel_id=1, replica_groups=mesh['row'=4,'col'=8] {'row','col'}, dimensions={0} | all-to-all | bytes 8192 | tf_op jit(solution)/shard_map/all_to_all | solution.py:98
  15.8 0.5 broadcast.51
  16.3 0.7 reduce.3
  17.0 0.1 reshape.81
  17.1 0.0 copy-done
  17.1 5.3 %gather_fusion = f32[1024,768]{1,0:T(8,128)} fusion(f32[512,768]{1,0:T(8,128)S(1)} %copy-done, s32[1024]{0:T(1024)S(1)} %broadcast_clamp_fusion), kind=kCustom, calls=%fused_computation | custom fusion | bytes 6295552 | tf_op jit(solution)/shard_map/jit(_take)/gather | solution.py:99
  22.4 0.0 copy-start.1
  22.4 3.7 %all-to-all-start.1 = ((f32[32,32,768]{2,1,0:T(8,128)}), f32[32,32,768]{2,1,0:T(8,128)}, u32[]{:S(2)}, u32[]{:S(2)}) async-start(f32[32,32,768]{2,1,0:T(8,128)} %bitcast.7), calls=%async_computation.1 | async-start | bytes 6291456 | tf_op jit(solution)/shard_map/all_to_all | solution.py:104
  26.1 0.0 copy-done.1
  26.1 0.1 iota_compare_fusion
  26.2 0.1 lt.32
  26.3 0.9 constant_dynamic-slice_fusion
  27.2 90.9 %all_gather.6 = f32[96,2,256]{2,1,0:T(2,128)S(1)} all-gather(f32[12,2,256]{2,1,0:T(2,128)S(1)} %constant_dynamic-slice_fusion), channel_id=1, replica_groups=mesh['row'=4,'col'=8] {'col'}, dimensions={0}, use_global_device_ids=true | all-gather | bytes 221184 | tf_op jit(solution)/shard_map/all_gather | solution.py:102
  118.0 8.5 %all_gather.7 = f32[96,8,256]{2,0,1:T(8,128)S(1)} all-gather(f32[96,2,256]{2,0,1:T(8,128)S(1)} %copy.8), channel_id=1, replica_groups=mesh['row'=4,'col'=8] {'row'}, dimensions={1}, use_global_device_ids=true | all-gather | bytes 983040 | tf_op jit(solution)/shard_map/all_gather | solution.py:103
  126.6 1.4 copy.10.cb_ref
  127.9 7.2 %build_table.1.w_ref = bf16[96,256,64]{2,1,0:T(8,128)(2,1)} custom-call(f32[96,8,256]{2,1,0:T(8,128)} %copy.10.cb_ref), custom_call_target="tpu_custom_call" | custom-call | flops 100000000 | bytes 20000000 | tf_op jit(solution)/shard_map/build_table/pallas_call | solution.py:107
  135.1 0.0 all-to-all-done.1
  135.1 33.4 %score.1 = (f32[1,1024]{1,0:T(1,128)}, f32[1,1024]{1,0:T(1,128)}) custom-call(f32[1024,768]{1,0:T(8,128)} %v_ref.1, f32[1024,768]{1,0:T(8,128)} %bitcast.3.c_ref, s32[96,1024]{1,0:T(8,128)} %bitcast.8, f32[96,8,256]{2,1,0:T(8,128)} %copy.10.cb_ref, bf16[96,256,64]{2,1,0:T(8,128)(2,1)} %build_table.1.w_ref), custom_call_target="tpu_custom_call" | custom-call | tf_op jit(solution)/shard_map/score/pallas_call | solution.py:118
  168.5 1.3 broadcast_select_fusion
  (3 shorter events, 0.0 us)
Async XLA Ops:
  0.6 16.5 %copy-start = (f32[512,768]{1,0:T(8,128)S(1)}, f32[512,768]{1,0:T(8,128)}, u32[]{:S(2)}) copy-start(f32[512,768]{1,0:T(8,128)} %param.10) | copy-start | bytes 4718596
  22.4 3.7 %copy-start.1 = (s32[1,32]{1,0:T(1,128)S(1)}, s32[1,32]{1,0:T(1,128)}, u32[]{:S(2)}) copy-start(s32[1,32]{1,0:T(1,128)} %param.9) | copy-start | bytes 388
  22.4 112.7 %all-to-all-start.1 = ((f32[32,32,768]{2,1,0:T(8,128)}), f32[32,32,768]{2,1,0:T(8,128)}, u32[]{:S(2)}, u32[]{:S(2)}) async-start(f32[32,32,768]{2,1,0:T(8,128)} %bitcast.7), calls=%async_computation.1 | async-start | bytes 6291456 | tf_op jit(solution)/shard_map/all_to_all | solution.py:104

commit v2 on v1

v2 whole, which is shorter than its diff:
```python
import functools

import jax
import jax.numpy as jnp
from jax import lax
from jax.experimental import pallas as pl
from jax.experimental.pallas import tpu as pltpu
from jax.sharding import PartitionSpec as P

F32 = jnp.float32
BF16 = jnp.bfloat16
DEPTH = 64


def split3(x):
    hi = x.astype(BF16).astype(F32)
    rest = x - hi
    mid = rest.astype(BF16).astype(F32)
    return hi, mid, rest - mid


def build_table(cb_ref, w_ref):
    sub_count, sub_width, code_count = cb_ref.shape

    def step(m, carry):
        c = cb_ref[m]
        hi, mid, lo = split3(-2.0 * c)
        norm = jnp.sum(c * c, axis=0, keepdims=True)
        nh, nm, nl = split3(norm)
        line = lax.broadcasted_iota(jnp.int32, c.shape, 0)
        norms = jnp.where(line == 0, nh, jnp.where(line == 1, nm, jnp.where(line == 2, nl, 0.0)))
        pieces = [hi, hi, hi, mid, mid, lo, norms, jnp.zeros_like(c)]
        w_ref[m] = jnp.concatenate(pieces, axis=0).T.astype(BF16)
        return carry

    lax.fori_loop(0, sub_count, step, 0, unroll=4)


def pick(row, code, sub_width):
    lanes = code.shape[1]
    outs = []
    for start in range(0, lanes, 128):
        idx = jnp.broadcast_to(code[:, start:start + 128], (sub_width, 128))
        low = jnp.bitwise_and(idx, 127)
        got = None
        for part in range(row.shape[1] // 128):
            piece = jnp.take_along_axis(
                row[:, part * 128:(part + 1) * 128], low, axis=1, mode="promise_in_bounds"
            )
            got = piece if got is None else jnp.where(idx >= part * 128, piece, got)
        outs.append(got)
    return jnp.concatenate(outs, axis=1)


def score(rt_ref, codes_ref, cb_ref, w_ref):
    sub_count, sub_width, code_count = cb_ref.shape
    width = rt_ref.shape[1]
    ones = jnp.ones((sub_width, width), F32)
    zeros = jnp.zeros((sub_width, width), F32)

    def step(g, carry):
        coded, norm, best = carry
        codes = codes_ref[pl.ds(pl.multiple_of(g * 8, 8), 8), :]
        for i in range(8):
            m = g * 8 + i
            r = rt_ref[pl.ds(pl.multiple_of(m * sub_width, sub_width), sub_width), :]
            hi, mid, lo = split3(r)
            x = jnp.concatenate([hi, mid, lo, hi, mid, hi, ones, zeros], axis=0).astype(BF16)
            table = jnp.dot(w_ref[m], x, preferred_element_type=F32)
            best = best + jnp.min(table, axis=0, keepdims=True)
            norm = norm + r * r
            diff = r - pick(cb_ref[m], codes[i:i + 1, :], sub_width)
            coded = coded + diff * diff
        return coded, norm, best

    coded, norm, best = lax.fori_loop(
        0, sub_count // 8, step, (zeros, zeros, jnp.zeros((1, width), F32))
    )
    coded = jnp.sum(coded, axis=0, keepdims=True)
    best = best + jnp.sum(norm, axis=0, keepdims=True)
    return coded, best


def exchange_kernel(row_count, col_count, wanted_ref, cb_ref, v_ref, codes_ref, coded_ref, best_ref,
                    got_ref, book_ref, w_ref, rt_ref, first_send, second_send, book_recv, rows_send, rows_recv):
    row = lax.axis_index("row")
    col = lax.axis_index("col")
    sub_local = cb_ref.shape[0]
    width = rt_ref.shape[1]
    capacity = width // col_count
    groups = col_count // row_count

    def other_row(step):
        return lax.rem(row + step + row_count, row_count)

    def other_col(step):
        return lax.rem(col + step + col_count, col_count)

    def piece(j):
        return book_ref.at[pl.ds(j * sub_local, sub_local)]

    def block(ref, r, c):
        start = pl.multiple_of((r * col_count + c) * capacity, capacity)
        return ref.at[pl.ds(start, capacity)]

    def first_copy(step):
        return pltpu.make_async_remote_copy(
            src_ref=cb_ref, dst_ref=piece(col), send_sem=first_send.at[step], recv_sem=book_recv.at[col],
            device_id=(row, other_col(step)), device_id_type=pl.DeviceIdType.MESH)

    def second_copy(group, step):
        j = group * row_count + row
        return pltpu.make_async_remote_copy(
            src_ref=piece(j), dst_ref=piece(j), send_sem=second_send.at[group, step], recv_sem=book_recv.at[j],
            device_id=(other_row(step), col), device_id_type=pl.DeviceIdType.MESH)

    def arrived(j):
        return pltpu.make_async_remote_copy(
            src_ref=cb_ref, dst_ref=piece(j), send_sem=first_send.at[0], recv_sem=book_recv.at[j],
            device_id=(row, other_col(1)), device_id_type=pl.DeviceIdType.MESH)

    def rows_copy(row_step, col_step):
        r, c = other_row(row_step), other_col(col_step)
        slot = row_step * col_count + col_step
        return pltpu.make_async_remote_copy(
            src_ref=block(wanted_ref, r, c), dst_ref=block(got_ref, row, col),
            send_sem=rows_send.at[slot], recv_sem=rows_recv.at[slot],
            device_id=(r, c), device_id_type=pl.DeviceIdType.MESH)

    def rows_arrived(row_step, col_step):
        r, c = other_row(-row_step), other_col(-col_step)
        slot = row_step * col_count + col_step
        return pltpu.make_async_remote_copy(
            src_ref=block(wanted_ref, r, c), dst_ref=block(got_ref, r, c),
            send_sem=rows_send.at[slot], recv_sem=rows_recv.at[slot],
            device_id=(other_row(row_step), other_col(col_step)), device_id_type=pl.DeviceIdType.MESH)

    spreads = lax.rem(col, row_count) == row

    @pl.when(spreads)
    def _():
        for step in range(1, col_count):
            first_copy(step).start()

    book_ref[pl.ds(col * sub_local, sub_local)] = cb_ref[...]
    own = pl.multiple_of((row * col_count + col) * capacity, capacity)
    got_ref[pl.ds(own, capacity), :] = wanted_ref[pl.ds(own, capacity), :]
    for group in range(groups):
        @pl.when(group * row_count + row != col)
        def _(group=group):
            arrived(group * row_count + row).wait_recv()
            for step in range(1, row_count):
                second_copy(group, step).start()

    pairs = [(a, b) for a in range(row_count) for b in range(col_count) if a + b > 0]
    for a, b in pairs:
        rows_copy(a, b).start()

    for group in range(groups):
        for step in range(1, row_count):
            j = group * row_count + other_row(-step)

            @pl.when(j != col)
            def _(j=j):
                arrived(j).wait_recv()
    build_table(book_ref, w_ref)

    for a in range(row_count):
        for b in range(col_count):
            if a + b > 0:
                rows_arrived(a, b).wait_recv()
        base = pl.multiple_of(other_row(-a) * width, width)
        rt_ref[...] = (v_ref[pl.ds(base, width), :] - got_ref[pl.ds(base, width), :]).T
        coded, best = score(rt_ref, codes_ref.at[:, pl.ds(base, width)], book_ref, w_ref)
        coded_ref[:, pl.ds(base, width)] = coded
        best_ref[:, pl.ds(base, width)] = best

    @pl.when(spreads)
    def _():
        for step in range(1, col_count):
            first_copy(step).wait_send()

    for group in range(groups):
        @pl.when(group * row_count + row != col)
        def _(group=group):
            for step in range(1, row_count):
                second_copy(group, step).wait_send()
    for a, b in pairs:
        rows_copy(a, b).wait_send()


def local(vectors, list_ids, pq_codes, fill_counts, centroids, codebook):
    row_count = lax.axis_size("row")
    col_count = lax.axis_size("col")
    device_count = row_count * col_count
    slot_count, feature_width = vectors.shape
    capacity = slot_count // device_count
    sub_total = pq_codes.shape[1]
    sub_width, code_count = codebook.shape[1:]
    axes = ("row", "col")
    swap = functools.partial(lax.all_to_all, axis_name=axes, split_axis=0, concat_axis=0, tiled=True)

    got_ids = swap(list_ids.reshape(device_count, capacity)).reshape(slot_count)
    wanted = jnp.take(centroids, got_ids % centroids.shape[0], axis=0, mode="clip")
    width = slot_count // row_count
    vmem = pl.BlockSpec(memory_space=pltpu.VMEM)
    coded, best = pl.pallas_call(
        functools.partial(exchange_kernel, row_count, col_count),
        out_shape=[jax.ShapeDtypeStruct((1, slot_count), F32)] * 2,
        in_specs=[vmem] * 4,
        out_specs=[vmem] * 2,
        scratch_shapes=[
            pltpu.VMEM((slot_count, feature_width), F32),
            pltpu.VMEM((sub_total, sub_width, code_count), F32),
            pltpu.VMEM((sub_total, code_count, DEPTH), BF16),
            pltpu.VMEM((feature_width, width), F32),
            pltpu.SemaphoreType.DMA((col_count,)),
            pltpu.SemaphoreType.DMA((col_count // row_count, row_count)),
            pltpu.SemaphoreType.DMA((col_count,)),
            pltpu.SemaphoreType.DMA((device_count,)),
            pltpu.SemaphoreType.DMA((device_count,)),
        ],
        compiler_params=pltpu.CompilerParams(has_side_effects=True, vmem_limit_bytes=48 * 2**20),
        name="exchange_score",
    )(wanted, codebook, vectors, pq_codes.T)

    slot_pos = jnp.arange(capacity, dtype=jnp.int32)
    live = (slot_pos[None, :] < fill_counts[0][:, None]).reshape(slot_count)
    coded_err = jnp.where(live, coded.reshape(slot_count), 0.0)
    best_err = jnp.where(live, best.reshape(slot_count), 0.0)
    return (coded_err, best_err)


def solution(mesh):
    in_specs = (
        P(("row", "col"), None),
        P(("row", "col")),
        P(("row", "col"), None),
        P(("row", "col"), None),
        P(("row", "col"), None),
        P("col", None, None),
    )
    out_specs = (P(("row", "col")), P(("row", "col")))
    return jax.shard_map(local, mesh=mesh, in_specs=in_specs, out_specs=out_specs, check_vma=False)
```

time: 170 us -> 112 us (0.66)
  the two profiles are of different devices: /device:TPU:0 before, /device:TPU:13 now
where the time goes in v2:
time: 112 us
  Pallas kernels  89.5 us (80%)
  local copies, waits for them, and re-layouts  9.36 us (8%)
  starting transfers between devices  6.27 us (6%)
  waiting for transfers between devices  3.96 us (4%)
  other arithmetic  2.04 us (2%)
    pallas_call x1, Pallas kernels, local(): pl.pallas_call(functools.partial(exchange_kernel, row_count, col_count),...  89.5 us
    all_to_all x1, starting transfers between devices, local(): got_ids = swap(list_ids.reshape(device_count, capacity)).reshape(slot_count)  6.27 us
    gather x1, local copies, waits for them, and re-layouts, local(): jnp.take(centroids, got_ids % centroids.shape[0], axis=0, mode='clip')  5.29 us
    all_to_all x1, waiting for transfers between devices, local(): got_ids = swap(list_ids.reshape(device_count, capacity)).reshape(slot_count)  3.96 us
  transfers between devices with their start and end apart: 1, of which 1 were waited for; matrix products, arithmetic and copies ran while one was open for 1% of the time, Pallas kernels for 0%

profile of v2, /device:TPU:13, one launch (start us, length us, event | category | flops | bytes accessed | tf_op | source)
XLA Modules:
  0.0 111.8 jit_solution(13299204103799797886)
XLA Ops:
  0.6 0.0 copy-start
  0.6 1.5 %all_to_all.6 = s32[32,1,32]{2,1,0:T(1,128)} reshape(s32[1024]{0:T(1024)} %param.7) | data formatting | bytes 8192 | tf_op jit(solution)/shard_map/all_to_all | solution.py:203
  2.1 6.3 %all-to-all-start = ((s32[32,1,32]{2,1,0:T(1,128)}), s32[32,1,32]{2,1,0:T(1,128)S(1)}, u32[]{:S(2)}, u32[]{:S(2)}) async-start(s32[32,1,32]{2,1,0:T(1,128)} %all_to_all.6), calls=%async_computation | async-start | bytes 32768 | tf_op jit(solution)/shard_map/all_to_all | solution.py:203
  8.4 0.7 iota_compare_fusion
  9.1 0.1 lt.29
  9.2 4.0 %all-to-all-done = s32[32,1,32]{2,1,0:T(1,128)S(1)} async-done(((s32[32,1,32]{2,1,0:T(1,128)}), s32[32,1,32]{2,1,0:T(1,128)S(1)}, u32[]{:S(2)}, u32[]{:S(2)}) %all-to-all-start) | async-done | bytes 4128 | tf_op jit(solution)/shard_map/all_to_all | solution.py:203
  13.2 0.5 broadcast.51
  13.7 0.7 reduce.3
  14.4 0.1 reshape.75
  14.5 0.0 copy-done
  14.5 0.0 copy-start.2
  14.5 0.0 copy-start.3
  14.5 5.3 %gather_fusion = f32[1024,768]{1,0:T(8,128)} fusion(f32[512,768]{1,0:T(8,128)S(1)} %copy-done, s32[1024]{0:T(1024)S(1)} %broadcast_clamp_fusion), kind=kCustom, calls=%fused_computation | custom fusion | bytes 6295552 | tf_op jit(solution)/shard_map/jit(_take)/gather | solution.py:204
  19.8 0.0 copy-done.2
  19.8 0.0 copy-done.3
  19.8 0.0 copy-start.1
  19.8 1.9 %copy-done.1 = f32[1024,768]{1,0:T(8,128)S(1)} copy-done((f32[1024,768]{1,0:T(8,128)S(1)}, f32[1024,768]{1,0:T(8,128)}, u32[]{:S(2)}) %copy-start.1) | copy-done | bytes 3145752
  21.7 89.5 %exchange_score.1 = (f32[1,1024]{1,0:T(1,128)S(1)}, f32[1,1024]{1,0:T(1,128)S(1)}) custom-call(f32[1024,768]{1,0:T(8,128)S(1)} %copy-done.1, f32[12,8,256]{2,1,0:T(8,128)S(1)} %copy-done.3, f32[1024,768]{1,0:T(8,128)} %v_ref.1, s32[96,1024]{1,0:T(8,128)S(1)} %bitcast.5), custom_call_target="tpu_custom_call" | custom-call | tf_op jit(solution)/shard_map/exchange_score/pallas_call | solution.py:207
  111.2 0.6 broadcast_select_fusion
  (2 shorter events, 0.0 us)
Async XLA Ops:
  0.6 13.9 %copy-start = (f32[512,768]{1,0:T(8,128)S(1)}, f32[512,768]{1,0:T(8,128)}, u32[]{:S(2)}) copy-start(f32[512,768]{1,0:T(8,128)} %param.10) | copy-start | bytes 4718596
  2.1 11.1 %all-to-all-start = ((s32[32,1,32]{2,1,0:T(1,128)}), s32[32,1,32]{2,1,0:T(1,128)S(1)}, u32[]{:S(2)}, u32[]{:S(2)}) async-start(s32[32,1,32]{2,1,0:T(1,128)} %all_to_all.6), calls=%async_computation | async-start | bytes 32768 | tf_op jit(solution)/shard_map/all_to_all | solution.py:203
  14.5 5.3 %copy-start.2 = (s32[1024,96]{0,1:T(8,128)S(1)}, s32[1024,96]{0,1:T(8,128)}, u32[]{:S(2)}) copy-start(s32[1024,96]{0,1:T(8,128)} %param.8) | copy-start | bytes 1179652
  14.5 5.3 %copy-start.3 = (f32[12,8,256]{2,1,0:T(8,128)S(1)}, f32[12,8,256]{2,1,0:T(8,128)}, u32[]{:S(2)}) copy-start(f32[12,8,256]{2,1,0:T(8,128)} %cb_ref.1) | copy-start | bytes 294916
  19.8 1.9 %copy-start.1 = (f32[1024,768]{1,0:T(8,128)S(1)}, f32[1024,768]{1,0:T(8,128)}, u32[]{:S(2)}) copy-start(f32[1024,768]{1,0:T(8,128)} %gather_fusion) | copy-start | bytes 9437188

commit v3 on v2

--- a/solution.py
+++ b/solution.py
@@ -189,6 +189,35 @@
         rows_copy(a, b).wait_send()
 
 
+def ids_kernel(row_count, col_count, ids_ref, out_ref, land_ref, send, recv):
+    row = lax.axis_index("row")
+    col = lax.axis_index("col")
+    me = row * col_count + col
+
+    def other(a, b):
+        return lax.rem(row + a + row_count, row_count), lax.rem(col + b + col_count, col_count)
+
+    def copy(a, b, back):
+        r, c = other(a, b)
+        fr, fc = other(-a, -b)
+        slot = a * col_count + b
+        return pltpu.make_async_remote_copy(
+            src_ref=ids_ref.at[r * col_count + c],
+            dst_ref=land_ref.at[fr * col_count + fc if back else me],
+            send_sem=send.at[slot], recv_sem=recv.at[slot],
+            device_id=(r, c), device_id_type=pl.DeviceIdType.MESH)
+
+    pairs = [(a, b) for a in range(row_count) for b in range(col_count) if a + b > 0]
+    for a, b in pairs:
+        copy(a, b, False).start()
+    land_ref[me] = ids_ref[me]
+    for a, b in pairs:
+        copy(a, b, True).wait_recv()
+    out_ref[...] = land_ref[...]
+    for a, b in pairs:
+        copy(a, b, False).wait_send()
+
+
 def local(vectors, list_ids, pq_codes, fill_counts, centroids, codebook):
     row_count = lax.axis_size("row")
     col_count = lax.axis_size("col")
@@ -197,13 +226,24 @@
     capacity = slot_count // device_count
     sub_total = pq_codes.shape[1]
     sub_width, code_count = codebook.shape[1:]
-    axes = ("row", "col")
-    swap = functools.partial(lax.all_to_all, axis_name=axes, split_axis=0, concat_axis=0, tiled=True)
-
-    got_ids = swap(list_ids.reshape(device_count, capacity)).reshape(slot_count)
-    wanted = jnp.take(centroids, got_ids % centroids.shape[0], axis=0, mode="clip")
+    vmem = pl.BlockSpec(memory_space=pltpu.VMEM)
+    ids_shape = (device_count, 1, capacity)
+    got_ids = pl.pallas_call(
+        functools.partial(ids_kernel, row_count, col_count),
+        out_shape=jax.ShapeDtypeStruct(ids_shape, jnp.int32),
+        in_specs=[vmem],
+        out_specs=vmem,
+        scratch_shapes=[
+            pltpu.VMEM(ids_shape, jnp.int32),
+            pltpu.SemaphoreType.DMA((device_count,)),
+            pltpu.SemaphoreType.DMA((device_count,)),
+        ],
+        compiler_params=pltpu.CompilerParams(has_side_effects=True),
+        name="exchange_ids",
+    )(list_ids.reshape(ids_shape)).reshape(slot_count)
+    lines = lax.rem(got_ids, centroids.shape[0])
+    wanted = centroids.at[lines].get(mode="promise_in_bounds", wrap_negative_indices=False)
     width = slot_count // row_count
-    vmem = pl.BlockSpec(memory_space=pltpu.VMEM)
     coded, best = pl.pallas_call(
         functools.partial(exchange_kernel, row_count, col_count),
         out_shape=[jax.ShapeDtypeStruct((1, slot_count), F32)] * 2,

time: 112 us -> 115 us (1.027)
  Pallas kernels: 89.5 us -> 102 us
  starting transfers between devices: 6.27 us -> 0 us
  waiting for transfers between devices: 3.96 us -> 0 us
    pallas_call x0 -> x1, Pallas kernels: none -> 12.8 us  [local(): pl.pallas_call(functools.partial(ids_kernel, row_count, col_count), out_s...]
    all_to_all x1 -> x0, starting transfers between devices: 6.27 us -> none  [local(): got_ids = swap(list_ids.reshape(device_count, capacity)).reshape(slot_count)]
    all_to_all x1 -> x0, waiting for transfers between devices: 3.96 us -> none  [local(): got_ids = swap(list_ids.reshape(device_count, capacity)).reshape(slot_count)]
    all_to_all x2 -> x0, local copies, waits for them, and re-layouts: 2 us -> none  [local(): got_ids = swap(list_ids.reshape(device_count, capacity)).reshape(slot_count)]
    reshape x1 -> x2, local copies, waits for them, and re-layouts: 0.08 us -> 1.57 us  [the longest x1 1.49 us: local(): list_ids.reshape(ids_shape)]
    pallas_call x0 -> x1, other arithmetic: none -> 1.41 us  [local(): pl.pallas_call(functools.partial(ids_kernel, row_count, col_count), out_s...]
  transfers between devices with their start and end apart: 1 -> 0, of which waited for: 1 -> 0; matrix products, arithmetic and copies ran while one was open for 1% -> 0% of each run, Pallas kernels for 0% -> 0%
where the time goes in v3:
time: 115 us; the launch traced here: 114 us
  Pallas kernels  102 us (89%)
  local copies, waits for them, and re-layouts  9.39 us (8%)
  other arithmetic  2.1 us (2%)
    pallas_call x1, Pallas kernels, local(): pl.pallas_call(functools.partial(exchange_kernel, row_count, col_count),...  89.5 us
    pallas_call x1, Pallas kernels, local(): pl.pallas_call(functools.partial(ids_kernel, row_count, col_count), out_s...  12.8 us
    gather x1, local copies, waits for them, and re-layouts, local(): centroids.at[lines]  5.31 us

profile of v3, /device:TPU:13, one launch (start us, length us, event | category | flops | bytes accessed | tf_op | source)
XLA Modules:
  0.0 114.5 jit_solution(11633390412046165306)
XLA Ops:
  0.6 0.0 copy-start
  0.6 1.5 %reshape.58.ids_ref = s32[32,1,32]{2,1,0:T(1,128)} reshape(s32[1024]{0:T(1024)} %param.7) | data formatting | bytes 8192 | tf_op jit(solution)/shard_map/reshape | solution.py:243
  2.1 12.8 %exchange_ids.1 = s32[32,1,32]{2,1,0:T(1,128)} custom-call(s32[32,1,32]{2,1,0:T(1,128)} %reshape.58.ids_ref), custom_call_target="tpu_custom_call" | custom-call | tf_op jit(solution)/shard_map/exchange_ids/pallas_call | solution.py:231
  15.0 0.5 broadcast.29
  15.5 1.4 %reduce.3 = s32[32,32]{1,0:T(8,128)S(1)} reduce(s32[32,1,32]{2,1,0:T(1,128)} %exchange_ids.1, s32[]{:T(128)} %broadcast.29), dimensions={1}, to_apply=%pallas_call.10.reduce_sub_computation.3 | reduce | bytes 8196 | tf_op jit(solution)/shard_map/exchange_ids/pallas_call | solution.py:231
  16.9 0.1 reshape.59
  17.0 0.0 copy-done
  17.0 0.0 copy-start.2
  17.0 0.0 copy-start.3
  17.0 5.3 %gather_fusion = f32[1024,768]{1,0:T(8,128)} fusion(f32[512,768]{1,0:T(8,128)S(1)} %copy-done, s32[1024]{0:T(1024)S(1)} %broadcast_clamp_fusion), kind=kCustom, calls=%fused_computation | custom fusion | bytes 6295552 | tf_op jit(solution)/shard_map/gather | solution.py:245
  22.4 0.0 copy-done.2
  22.4 0.0 copy-done.3
  22.4 0.0 copy-start.1
  22.4 1.9 %copy-done.1 = f32[1024,768]{1,0:T(8,128)S(1)} copy-done((f32[1024,768]{1,0:T(8,128)S(1)}, f32[1024,768]{1,0:T(8,128)}, u32[]{:S(2)}) %copy-start.1) | copy-done | bytes 3145752
  24.2 0.0 copy-start.4
  24.2 89.5 %exchange_score.1 = (f32[1,1024]{1,0:T(1,128)S(1)}, f32[1,1024]{1,0:T(1,128)S(1)}) custom-call(f32[1024,768]{1,0:T(8,128)S(1)} %copy-done.1, f32[12,8,256]{2,1,0:T(8,128)S(1)} %copy-done.3, f32[1024,768]{1,0:T(8,128)} %v_ref.1, s32[96,1024]{1,0:T(8,128)S(1)} %bitcast.5), custom_call_target="tpu_custom_call" | custom-call | tf_op jit(solution)/shard_map/exchange_score/pallas_call | solution.py:247
  113.7 0.0 copy-done.4
  113.7 0.1 iota_compare_fusion
  113.8 0.1 lt.23
  113.9 0.6 broadcast_select_fusion
  (2 shorter events, 0.0 us)
Async XLA Ops:
  0.6 16.4 %copy-start = (f32[512,768]{1,0:T(8,128)S(1)}, f32[512,768]{1,0:T(8,128)}, u32[]{:S(2)}) copy-start(f32[512,768]{1,0:T(8,128)} %param.10) | copy-start | bytes 4718596
  17.0 5.3 %copy-start.2 = (s32[1024,96]{0,1:T(8,128)S(1)}, s32[1024,96]{0,1:T(8,128)}, u32[]{:S(2)}) copy-start(s32[1024,96]{0,1:T(8,128)} %param.8) | copy-start | bytes 1179652
  17.0 5.3 %copy-start.3 = (f32[12,8,256]{2,1,0:T(8,128)S(1)}, f32[12,8,256]{2,1,0:T(8,128)}, u32[]{:S(2)}) copy-start(f32[12,8,256]{2,1,0:T(8,128)} %cb_ref.1) | copy-start | bytes 294916
  22.4 1.9 %copy-start.1 = (f32[1024,768]{1,0:T(8,128)S(1)}, f32[1024,768]{1,0:T(8,128)}, u32[]{:S(2)}) copy-start(f32[1024,768]{1,0:T(8,128)} %gather_fusion) | copy-start | bytes 9437188
  24.2 89.5 %copy-start.4 = (s32[1,32]{1,0:T(1,128)S(1)}, s32[1,32]{1,0:T(1,128)}, u32[]{:S(2)}) copy-start(s32[1,32]{1,0:T(1,128)} %param.9) | copy-start | bytes 388
